TPU v7x, 32 devices: a whole 2x2x4 slice. The times are simulated.
32 devices in a mesh: up: 8 (over y, x, core), dn: 4 (over z).
Axes of the slice: x: 2, y: 2, z: 4, core: 2. Of those that a mesh axis runs over, the one named last changes fastest.
Arguments:
- start_vector: bfloat16 [13312, 13312], P('up', 'dn'), may hold values from -6 to 6
- hop_tiles: bfloat16 [104, 5, 128, 128], replicated, may hold values from -0.5 to 0.5
- tile_columns: int32 [104, 5], replicated, may hold values from 0 to 103, as said below
- tile_signs: int32 [104, 5], replicated, may hold values from 0 to 1
- occupation: int32 [16, 13312], replicated, may hold values from 0 to 1, as said below
Outputs:
- next_vector: bfloat16 [13312, 13312], P('up', 'dn')
- alphas: float32 [2], replicated
- betas: float32 [2], replicated
Inputs may be any that keep to these rules, and one draw needn't show every extreme that they name: Each row of tile_columns names 5 different tile columns. Every column of occupation holds exactly 8 ones.
All inputs are finite; a program needn't handle non-finite values.
Results may differ from a plain program's by a relative error of at most 0.0065.
Values may be sent and summed in bfloat16 or wider, within the bound.
A program may use at most 256 MiB of HBM per device.

v0:
```python
import jax
import jax.numpy as jnp
from jax import lax
from jax.sharding import PartitionSpec as P

STEPS = 2
coupling = 4.0


def hop_lead(matrix, signed, tile_columns):
    layout = matrix.shape
    tile_width = signed.shape[-1]
    cube = matrix.reshape(layout[0] // tile_width, tile_width, -1)
    picked = cube[tile_columns]
    result = jnp.einsum("ikab,ikbm->iam", signed, picked, preferred_element_type=jnp.float32)
    return result.reshape(layout).astype(jnp.bfloat16)


def body(start_vector, hop_tiles, tile_columns, tile_signs, occupation):
    signed = hop_tiles * (1 - 2 * tile_signs).astype(jnp.bfloat16)[:, :, None, None]
    rows_local, cols_local = start_vector.shape
    count_up = lax.axis_size("up")
    count_down = lax.axis_size("dn")
    row_start = lax.axis_index("up") * rows_local
    col_start = lax.axis_index("dn") * cols_local
    block_rows, block_cols = start_vector.shape
    occ_rows = lax.dynamic_slice_in_dim(occupation, row_start, block_rows, 1).astype(jnp.bfloat16)
    occ_cols = lax.dynamic_slice_in_dim(occupation, col_start, block_cols, 1).astype(jnp.bfloat16)
    diagonal = coupling * jnp.einsum(
        "sa,sb->ab", occ_rows, occ_cols, preferred_element_type=jnp.float32
    )
    vector = start_vector.astype(jnp.float32)
    total = lax.psum(jnp.sum(vector * vector), ("up", "dn"))
    vector = vector / jnp.maximum(jnp.sqrt(total), 1.0)
    length = total / jnp.maximum(total, 1.0)
    previous = jnp.zeros_like(vector)
    beta_value = jnp.float32(0.0)
    alpha_list = []
    beta_list = []
    for iteration in range(STEPS):
        rounded = vector.astype(jnp.bfloat16)
        cube = rounded.reshape(block_rows, count_up, block_cols // count_up)
        up_part = lax.all_to_all(cube, "up", split_axis=1, concat_axis=0, tiled=True)
        up_whole = up_part.reshape(up_part.shape[0], up_part.shape[2])
        up_hopped = hop_lead(up_whole, signed, tile_columns).reshape(up_part.shape)
        moved = lax.all_to_all(up_hopped, "up", split_axis=0, concat_axis=1, tiled=True)
        hopped_up = moved.reshape(block_rows, block_cols)
        flipped = rounded.T.reshape(block_cols, count_down, block_rows // count_down)
        part = lax.all_to_all(flipped, "dn", split_axis=1, concat_axis=0, tiled=True)
        whole = part.reshape(part.shape[0], part.shape[2])
        hopped = hop_lead(whole, signed, tile_columns).reshape(part.shape)
        returned = lax.all_to_all(hopped, "dn", split_axis=0, concat_axis=1, tiled=True)
        hopped_down = returned.reshape(block_cols, block_rows).T
        work = (
            hopped_up.astype(jnp.float32)
            + hopped_down.astype(jnp.float32)
            + diagonal * vector
            - beta_value * previous
        )
        intersect, square = lax.psum((jnp.sum(work * vector), jnp.sum(work * work)), ("up", "dn"))
        work = work - intersect * vector
        residual = square - 2.0 * intersect * intersect + intersect * intersect * length
        beta_value = jnp.sqrt(jnp.maximum(residual, 1.0))
        length = residual / jnp.maximum(residual, 1.0)
        previous = vector
        vector = work / beta_value
        alpha_list.append(intersect)
        beta_list.append(beta_value)
    final = vector.astype(jnp.bfloat16)
    return (final, jnp.stack(alpha_list), jnp.stack(beta_list))


def solution(mesh):
    placed = (P("up", "dn"), P(), P(), P(), P())
    return jax.shard_map(
        body, mesh=mesh, in_specs=placed, out_specs=(P("up", "dn"), P(), P()), check_vma=False
    )
```

profile of v0, /device:TPU:12, one launch (start us, length us, event | category | flops | bytes accessed | tf_op | source)
XLA Modules:
  0.0 2605.0 jit_solution(15196336587195113989)
XLA Ops:
  11.1 41.6 %psum.35 = f32[]{:T(128)} all-reduce(f32[]{:T(128)} %fusion), channel_id=1, replica_groups=mesh['up'=8,'dn'=4] {'up','dn'}, use_global_device_ids=true, to_apply=%region_1.0 | all-reduce | flops 1 | bytes 8 | tf_op jit(solution)/shard_map/psum | solution.py:33
  80.3 127.1 %all_to_all.96 = bf16[1664,8,416]{0,2,1:T(8,128)(2,1)} all-to-all(bf16[1664,8,416]{0,2,1:T(8,128)(2,1)} %bitcast.112), channel_id=1, replica_groups=mesh['up'=8,'dn'=4] {'up'}, dimensions={1} | all-to-all | bytes 22151168 | tf_op jit(solution)/shard_map/all_to_all | solution.py:43
  233.4 21.0 reshape_reshape.12
  265.2 26.4 %gather_fusion = bf16[520,128,416]{1,2,0:T(8,128)(2,1)} fusion(bf16[104,128,416]{1,2,0:T(8,128)(2,1)} %copy.65, s32[1024]{0:T(1024)S(1)} %pad_clamp_fusion), kind=kCustom, calls=%fused_computation | custom fusion | bytes 110757920 | tf_op jit(solution)/shard_map/gather | solution.py:14
  291.6 29.5 %bitcast_convert_fusion.3 = bf16[104,128,416]{1,2,0:T(8,128)(2,1)} fusion(bf16[104,5,128,416]{2,3,1,0:T(8,128)(2,1)} %bitcast.107, bf16[104,5,128,128]{3,2,1,0:T(8,128)(2,1)} %param.6, bf16[104,5]{1,0:T(8,128)(2,1)S(1)} %copy.61), kind=kOutput, calls=%fused_computation.15 | convolution fusion | flops 7102431232 | bytes 83493904 | tf_op jit(solution)/shard_map/ikab,ikbm->iam/dot_general | solution.py:15
  337.4 77.7 %reshape.155 = bf16[13312,1,416]{2,1,0:T(2,128)(2,1)} reshape(bf16[104,128,416]{2,1,0:T(8,128)(2,1)} %copy.95) | data formatting | bytes 22151168 | tf_op jit(solution)/shard_map/convert_element_type | solution.py:16
  415.7 87.5 %reduce = bf16[13312,416]{1,0:T(8,128)(2,1)} reduce(bf16[13312,1,416]{2,1,0:T(2,128)(2,1)} %reshape.155, bf16[]{:T(256)} %broadcast.21), dimensions={1}, to_apply=%reshape.155.reduce_sub_computation | reduce | bytes 22151170 | tf_op jit(solution)/shard_map/convert_element_type | solution.py:16
  503.1 21.7 reshape.159
  531.9 26.0 copy.70
  587.4 26.4 %gather_fusion.1 = bf16[520,128,416]{1,2,0:T(8,128)(2,1)} fusion(bf16[104,128,416]{1,2,0:T(8,128)(2,1)} %copy.71, s32[1024]{0:T(1024)S(1)} %pad_clamp_fusion), kind=kCustom, calls=%fused_computation.1 | custom fusion | bytes 110757920 | tf_op jit(solution)/shard_map/gather | solution.py:14
  613.8 29.4 %bitcast_convert_fusion.2 = bf16[104,128,416]{1,2,0:T(8,128)(2,1)} fusion(bf16[104,5,128,416]{2,3,1,0:T(8,128)(2,1)} %bitcast.108, bf16[104,5,128,128]{3,2,1,0:T(8,128)(2,1)} %param.6, bf16[104,5]{1,0:T(8,128)(2,1)S(1)} %copy.61), kind=kOutput, calls=%fused_computation.14 | convolution fusion | flops 7102431232 | bytes 83493904 | tf_op jit(solution)/shard_map/ikab,ikbm->iam/dot_general | solution.py:15
  659.6 77.6 %reshape.156 = bf16[13312,1,416]{2,1,0:T(2,128)(2,1)} reshape(bf16[104,128,416]{2,1,0:T(8,128)(2,1)} %copy.96) | data formatting | bytes 22151168 | tf_op jit(solution)/shard_map/convert_element_type | solution.py:16
  737.1 87.6 %reduce.1 = bf16[13312,416]{1,0:T(8,128)(2,1)} reduce(bf16[13312,1,416]{2,1,0:T(2,128)(2,1)} %reshape.156, bf16[]{:T(256)} %broadcast.21), dimensions={1}, to_apply=%reshape.156.reduce_sub_computation | reduce | bytes 22151170 | tf_op jit(solution)/shard_map/convert_element_type | solution.py:16
  824.8 22.4 reshape.161
  854.8 30.4 %reshape.160 = bf16[13312,1,416]{2,1,0:T(2,128)(2,1)} reshape(bf16[8,2,346112]{2,1,0:T(2,128)(2,1)} %all-to-all-done.1) | data formatting | bytes 22151168
  885.3 52.5 %copy.68 = bf16[13312,1,416]{0,2,1:T(8,128)(2,1)} copy(bf16[13312,1,416]{2,1,0:T(2,128)(2,1)} %reshape.160) | data formatting | bytes 22151168 | tf_op jit(solution)/shard_map/all_to_all | solution.py:46
  972.4 22.9 copy.76
  995.2 96.4 %all-to-all-done.3 = bf16[4,2,692224]{2,1,0:T(2,128)(2,1)} async-done(((bf16[4,2,692224]{2,1,0:T(2,128)(2,1)}), bf16[4,2,692224]{2,1,0:T(2,128)(2,1)}, u32[]{:S(2)}, u32[]{:S(2)}) %all-to-all-start.3) | async-done | bytes 11075616 | tf_op jit(solution)/shard_map/all_to_all | solution.py:52
  1091.6 45.3 %reshape.162 = bf16[13312,1,416]{2,1,0:T(2,128)(2,1)} reshape(bf16[4,2,692224]{2,1,0:T(2,128)(2,1)} %all-to-all-done.3) | data formatting | bytes 22151168
  1136.9 52.8 %copy.74 = bf16[13312,1,416]{0,2,1:T(8,128)(2,1)} copy(bf16[13312,1,416]{2,1,0:T(2,128)(2,1)} %reshape.162) | data formatting | bytes 22151168 | tf_op jit(solution)/shard_map/all_to_all | solution.py:52
  1189.8 21.5 reshape.109
  1211.3 19.4 copy.75
  1230.7 32.3 %multiply_reduce_fusion.3 = (f32[]{:T(128)}, f32[]{:T(128)}, f32[1664,3328]{1,0:T(8,128)}, f32[1664,3328]{1,0:T(8,128)}) fusion(f32[]{:T(128)S(6)} %max.13, bf16[1664,3328]{1,0:T(8,128)(2,1)} %param.5, f32[1664,3328]{1,0:T(8,128)} %copy.76, f32[3328,4,1,416]{0,3,1,2:T(8,128)} %copy.75, s32[16,13312]{1,0:T(8,128)} %param.9, s32[]{:T(128)S(6)} %select_n.14, ...), kind=kOutput, calls=%fused_computation.21 | convolution fusion | flops 232667136 | bytes 99999760 | tf_op jit(solution)/shard_map/sa,sb->ab/dot_general | solution.py:29
  1263.1 43.3 %all-reduce.1 = (f32[]{:T(128)}, f32[]{:T(128)}) all-reduce(f32[]{:T(128)} %get-tuple-element.6, f32[]{:T(128)} %get-tuple-element.5), channel_id=1, replica_groups=mesh['up'=8,'dn'=4] {'up','dn'}, use_global_device_ids=true, to_apply=%region_5.0 | all-reduce | flops 2 | bytes 16 | tf_op jit(solution)/shard_map/psum | solution.py:60
  1309.6 22.7 fusion.28
  1348.6 127.0 %all_to_all.97 = bf16[1664,8,416]{0,2,1:T(8,128)(2,1)} all-to-all(bf16[1664,8,416]{0,2,1:T(8,128)(2,1)} %bitcast.113), channel_id=1, replica_groups=mesh['up'=8,'dn'=4] {'up'}, dimensions={1} | all-to-all | bytes 22151168 | tf_op jit(solution)/shard_map/all_to_all | solution.py:43
  1500.6 21.0 reshape_reshape.14
  1532.3 26.5 %gather_fusion.2 = bf16[520,128,416]{1,2,0:T(8,128)(2,1)} fusion(bf16[104,128,416]{1,2,0:T(8,128)(2,1)} %copy.79, s32[1024]{0:T(1024)S(1)} %copy-done.1), kind=kCustom, calls=%fused_computation.2 | custom fusion | bytes 110757920 | tf_op jit(solution)/shard_map/gather | solution.py:14
  1558.8 29.4 %bitcast_convert_fusion.1 = bf16[104,128,416]{1,2,0:T(8,128)(2,1)} fusion(bf16[104,5,128,416]{2,3,1,0:T(8,128)(2,1)} %bitcast.109, bf16[104,5,128,128]{3,2,1,0:T(8,128)(2,1)} %param.6, bf16[104,5]{1,0:T(8,128)(2,1)S(1)} %copy-done.3), kind=kOutput, calls=%fused_computation.13 | convolution fusion | flops 7102431232 | bytes 83493904 | tf_op jit(solution)/shard_map/ikab,ikbm->iam/dot_general | solution.py:15
  1604.5 77.7 %reshape.157 = bf16[13312,1,416]{2,1,0:T(2,128)(2,1)} reshape(bf16[104,128,416]{2,1,0:T(8,128)(2,1)} %copy.97) | data formatting | bytes 22151168 | tf_op jit(solution)/shard_map/convert_element_type | solution.py:16
  1682.3 87.5 %reduce.2 = bf16[13312,416]{1,0:T(8,128)(2,1)} reduce(bf16[13312,1,416]{2,1,0:T(2,128)(2,1)} %reshape.157, bf16[]{:T(256)} %broadcast.21), dimensions={1}, to_apply=%reshape.157.reduce_sub_computation | reduce | bytes 22151170 | tf_op jit(solution)/shard_map/convert_element_type | solution.py:16
  1769.7 21.7 reshape.163
  1798.5 26.0 copy.84
  1854.0 26.4 %gather_fusion.3 = bf16[520,128,416]{1,2,0:T(8,128)(2,1)} fusion(bf16[104,128,416]{1,2,0:T(8,128)(2,1)} %copy.85, s32[1024]{0:T(1024)S(1)} %copy-done.1), kind=kCustom, calls=%fused_computation.3 | custom fusion | bytes 110757920 | tf_op jit(solution)/shard_map/gather | solution.py:14
  1880.4 29.4 %bitcast_convert_fusion = bf16[104,128,416]{1,2,0:T(8,128)(2,1)} fusion(bf16[104,5,128,416]{2,3,1,0:T(8,128)(2,1)} %bitcast.106, bf16[104,5,128,128]{3,2,1,0:T(8,128)(2,1)} %param.6, bf16[104,5]{1,0:T(8,128)(2,1)S(1)} %copy-done.3), kind=kOutput, calls=%fused_computation.12 | convolution fusion | flops 7102431232 | bytes 83493904 | tf_op jit(solution)/shard_map/ikab,ikbm->iam/dot_general | solution.py:15
  1926.1 77.6 %reshape.158 = bf16[13312,1,416]{2,1,0:T(2,128)(2,1)} reshape(bf16[104,128,416]{2,1,0:T(8,128)(2,1)} %copy.98) | data formatting | bytes 22151168 | tf_op jit(solution)/shard_map/convert_element_type | solution.py:16
  2003.7 87.6 %reduce.3 = bf16[13312,416]{1,0:T(8,128)(2,1)} reduce(bf16[13312,1,416]{2,1,0:T(2,128)(2,1)} %reshape.158, bf16[]{:T(256)} %broadcast.21), dimensions={1}, to_apply=%reshape.158.reduce_sub_computation | reduce | bytes 22151170 | tf_op jit(solution)/shard_map/convert_element_type | solution.py:16
  2091.3 22.4 reshape.165
  2120.1 30.4 %reshape.164 = bf16[13312,1,416]{2,1,0:T(2,128)(2,1)} reshape(bf16[8,2,346112]{2,1,0:T(2,128)(2,1)} %all-to-all-done.5) | data formatting | bytes 22151168
  2150.5 52.5 %copy.82 = bf16[13312,1,416]{0,2,1:T(8,128)(2,1)} copy(bf16[13312,1,416]{2,1,0:T(2,128)(2,1)} %reshape.164) | data formatting | bytes 22151168 | tf_op jit(solution)/shard_map/all_to_all | solution.py:46
  2237.6 22.9 copy.90
  2260.5 97.7 %all-to-all-done.7 = bf16[4,2,692224]{2,1,0:T(2,128)(2,1)} async-done(((bf16[4,2,692224]{2,1,0:T(2,128)(2,1)}), bf16[4,2,692224]{2,1,0:T(2,128)(2,1)}, u32[]{:S(2)}, u32[]{:S(2)}) %all-to-all-start.7) | async-done | bytes 11075616 | tf_op jit(solution)/shard_map/all_to_all | solution.py:52
  2358.2 45.3 %reshape.166 = bf16[13312,1,416]{2,1,0:T(2,128)(2,1)} reshape(bf16[4,2,692224]{2,1,0:T(2,128)(2,1)} %all-to-all-done.7) | data formatting | bytes 22151168
  2403.5 52.7 %copy.88 = bf16[13312,1,416]{0,2,1:T(8,128)(2,1)} copy(bf16[13312,1,416]{2,1,0:T(2,128)(2,1)} %reshape.166) | data formatting | bytes 22151168 | tf_op jit(solution)/shard_map/all_to_all | solution.py:52
  2456.2 21.5 reshape.110
  2497.1 40.2 %multiply_reduce_fusion.1 = (f32[]{:T(128)}, f32[]{:T(128)}, f32[1664,3328]{1,0:T(8,128)}) fusion(f32[1664,3328]{1,0:T(8,128)} %get-tuple-element.13, f32[]{:T(128)S(6)} %max.13, bf16[1664,3328]{1,0:T(8,128)(2,1)} %param.5, f32[]{:T(128)} %sqrt.10, f32[1664,3328]{1,0:T(8,128)} %get-tuple-element.15, f32[1664,3328]{1,0:T(8,128)} %copy.90, ...), kind=kLoop, calls=%fused_computation.18 | loop fusion | flops 66453504 | bytes 121831440 | tf_op jit(solution)/shard_map/reduce_sum | solution.py:60
  2537.3 42.5 %all-reduce = (f32[]{:T(128)}, f32[]{:T(128)}) all-reduce(f32[]{:T(128)} %get-tuple-element.4, f32[]{:T(128)} %get-tuple-element.3), channel_id=1, replica_groups=mesh['up'=8,'dn'=4] {'up','dn'}, use_global_device_ids=true, to_apply=%region_9.0 | all-reduce | flops 2 | bytes 16 | tf_op jit(solution)/shard_map/psum | solution.py:60
  2583.3 19.5 divide_convert_fusion
  (53 shorter events, 368.2 us)
Async XLA Ops:
  80.3 133.9 %copy-start.4 = (s32[104,5]{0,1:T(8,128)S(1)}, s32[104,5]{0,1:T(8,128)}, u32[]{:S(2)}) copy-start(s32[104,5]{0,1:T(8,128)} %param.8) | copy-start | bytes 6244
  80.3 134.0 %copy-start.5 = (s32[104,5]{0,1:T(8,128)S(1)}, s32[104,5]{0,1:T(8,128)}, u32[]{:S(2)}) copy-start(s32[104,5]{0,1:T(8,128)} %param.7) | copy-start | bytes 6244
  207.5 317.4 %all-to-all-start.2 = ((bf16[3328,4,416]{0,2,1:T(8,128)(2,1)}), bf16[3328,4,416]{0,2,1:T(8,128)(2,1)}, u32[]{:S(2)}, u32[]{:S(2)}) async-start(bf16[3328,4,416]{0,2,1:T(8,128)(2,1)} %bitcast.96), calls=%async_computation.2 | async-start | bytes 22151168 | tf_op jit(solution)/shard_map/all_to_all | solution.py:49
  214.3 399.5 %copy-start.2 = (bf16[104,5]{1,0:T(8,128)(2,1)}, bf16[104,5]{1,0:T(8,128)(2,1)S(1)}, u32[]{:S(2)}) copy-start(bf16[104,5]{1,0:T(8,128)(2,1)S(1)} %copy.61) | copy-start | bytes 3124
  214.7 372.7 %copy-start = (s32[1024]{0:T(1024)}, s32[1024]{0:T(1024)S(1)}, u32[]{:S(2)}) copy-start(s32[1024]{0:T(1024)S(1)} %pad_clamp_fusion) | copy-start | bytes 12292
  524.9 322.3 %all-to-all-start.1 = ((bf16[8,2,346112]{2,1,0:T(2,128)(2,1)}), bf16[8,2,346112]{2,1,0:T(2,128)(2,1)}, u32[]{:S(2)}, u32[]{:S(2)}) async-start(bf16[8,2,346112]{2,1,0:T(2,128)(2,1)} %reshape.159), calls=%async_computation.1 | async-start | bytes 22151168 | tf_op jit(solution)/shard_map/all_to_all | solution.py:46
  847.2 244.5 %all-to-all-start.3 = ((bf16[4,2,692224]{2,1,0:T(2,128)(2,1)}), bf16[4,2,692224]{2,1,0:T(2,128)(2,1)}, u32[]{:S(2)}, u32[]{:S(2)}) async-start(bf16[4,2,692224]{2,1,0:T(2,128)(2,1)} %reshape.161), calls=%async_computation.3 | async-start | bytes 22151168 | tf_op jit(solution)/shard_map/all_to_all | solution.py:52
  1475.6 315.9 %all-to-all-start.6 = ((bf16[3328,4,416]{0,2,1:T(8,128)(2,1)}), bf16[3328,4,416]{0,2,1:T(8,128)(2,1)}, u32[]{:S(2)}, u32[]{:S(2)}) async-start(bf16[3328,4,416]{0,2,1:T(8,128)(2,1)} %bitcast.97), calls=%async_computation.6 | async-start | bytes 22151168 | tf_op jit(solution)/shard_map/all_to_all | solution.py:49
  1500.6 31.8 %copy-start.1 = (s32[1024]{0:T(1024)S(1)}, s32[1024]{0:T(1024)}, u32[]{:S(2)}) copy-start(s32[1024]{0:T(1024)} %copy-done) | copy-start | bytes 12292
  1532.3 26.5 %copy-start.3 = (bf16[104,5]{1,0:T(8,128)(2,1)S(1)}, bf16[104,5]{1,0:T(8,128)(2,1)}, u32[]{:S(2)}) copy-start(bf16[104,5]{1,0:T(8,128)(2,1)} %copy-done.2) | copy-start | bytes 3124
  1791.5 322.3 %all-to-all-start.5 = ((bf16[8,2,346112]{2,1,0:T(2,128)(2,1)}), bf16[8,2,346112]{2,1,0:T(2,128)(2,1)}, u32[]{:S(2)}, u32[]{:S(2)}) async-start(bf16[8,2,346112]{2,1,0:T(2,128)(2,1)} %reshape.163), calls=%async_computation.5 | async-start | bytes 22151168 | tf_op jit(solution)/shard_map/all_to_all | solution.py:46
  2113.7 244.5 %all-to-all-start.7 = ((bf16[4,2,692224]{2,1,0:T(2,128)(2,1)}), bf16[4,2,692224]{2,1,0:T(2,128)(2,1)}, u32[]{:S(2)}, u32[]{:S(2)}) async-start(bf16[4,2,692224]{2,1,0:T(2,128)(2,1)} %reshape.165), calls=%async_computation.7 | async-start | bytes 22151168 | tf_op jit(solution)/shard_map/all_to_all | solution.py:52
where the time goes:
time: 2630 us; the launch traced here: 2600 us
  local copies, waits for them, and re-layouts  1360 us (52%)
  other arithmetic  469 us (18%)
  blocking collectives  381 us (14%)
  waiting for transfers between devices  194 us (7%)
  matrix products  150 us (6%)
  starting transfers between devices  39.6 us (2%)
    convert_element_type x9, local copies, waits for them, and re-layouts, hop_lead(): return result.reshape(layout).astype(jnp.bfloat16)  376 us
    convert_element_type x4, other arithmetic, hop_lead(): return result.reshape(layout).astype(jnp.bfloat16)  350 us
    unnamed x22, local copies, waits for them, and re-layouts  257 us
    all_to_all x2, blocking collectives, body(): lax.all_to_all(cube, 'up', split_axis=1, concat_axis=0, tiled=True)  254 us
    all_to_all x2, waiting for transfers between devices, body(): lax.all_to_all(hopped, 'dn', split_axis=0, concat_axis=1, tiled=True)  194 us
    another operation x8, local copies, waits for them, and re-layouts, hop_lead(): cube = matrix.reshape(layout[0] // tile_width, tile_width, -1)  122 us
    dot_general x4, matrix products, hop_lead(): jnp.einsum('ikab,ikbm->iam', signed, picked, preferred_element_type=jnp.f...  118 us
    gather x4, local copies, waits for them, and re-layouts, hop_lead(): picked = cube[tile_columns]  106 us
  transfers between devices with their start and end apart: 6, of which 2 were waited for; matrix products, arithmetic and copies ran while one was open for 59% of the time, Pallas kernels for 0%

commit v1 on v0

--- a/solution.py
+++ b/solution.py
@@ -5,6 +5,28 @@
 
 STEPS = 2
 coupling = 4.0
+
+
+def split_up(shard, dim, length):
+    before, after = (shard.shape[:dim], shard.shape[dim + 1 :])
+    return jnp.moveaxis(shard.reshape(*before, length, -1, *after), dim, 0)
+
+
+def laid_out(blocks, dim):
+    blocks = jnp.moveaxis(blocks, 0, dim)
+    shape = blocks.shape
+    return blocks.reshape(*shape[:dim], shape[dim] * shape[dim + 1], *shape[dim + 2 :])
+
+
+def exchange_in_pairs(x, axis, split_dim, concat_dim):
+    size, position = (lax.axis_size(axis), lax.axis_index(axis))
+    blocks = split_up(x, split_dim, size)
+    gathered = [blocks[position]]
+    for step in range(1, size):
+        sent = blocks[position ^ step]
+        gathered.append(lax.ppermute(sent, axis, [(i, i ^ step) for i in range(size)]))
+    blocks = jnp.stack(gathered)[position ^ jnp.arange(size)]
+    return laid_out(blocks, concat_dim)
 
 
 def hop_lead(matrix, signed, tile_columns):
@@ -49,7 +71,7 @@
         part = lax.all_to_all(flipped, "dn", split_axis=1, concat_axis=0, tiled=True)
         whole = part.reshape(part.shape[0], part.shape[2])
         hopped = hop_lead(whole, signed, tile_columns).reshape(part.shape)
-        returned = lax.all_to_all(hopped, "dn", split_axis=0, concat_axis=1, tiled=True)
+        returned = exchange_in_pairs(hopped, "dn", 0, 1)
         hopped_down = returned.reshape(block_cols, block_rows).T
         work = (
             hopped_up.astype(jnp.float32)

time: 2630 us -> 2480 us (0.943)
  local copies, waits for them, and re-layouts: 1360 us -> 1120 us
  waiting for transfers between devices: 194 us -> 387 us
  other arithmetic: 469 us -> 375 us
    all_to_all x2, waiting for transfers between devices: 0.01 us -> 321 us  [body(): lax.all_to_all(flipped, 'dn', split_axis=1, concat_axis=0, tiled=True)]
    all_to_all x2 -> x0, waiting for transfers between devices: 194 us -> none  [body(): lax.all_to_all(hopped, 'dn', split_axis=0, concat_axis=1, tiled=True)]
    convert_element_type x4 -> x2, other arithmetic: 350 us -> 175 us  [hop_lead(): return result.reshape(layout).astype(jnp.bfloat16)]
    unnamed x22 -> x34, local copies, waits for them, and re-layouts: 257 us -> 140 us
    convert_element_type x9, local copies, waits for them, and re-layouts: 376 us -> 266 us  [hop_lead(): return result.reshape(layout).astype(jnp.bfloat16)]
    all_to_all x2 -> x0, local copies, waits for them, and re-layouts: 106 us -> none  [body(): lax.all_to_all(hopped, 'dn', split_axis=0, concat_axis=1, tiled=True)]
    convert_element_type x4 -> x0, local copies, waits for them, and re-layouts: 81.9 us -> none  [body(): hopped_down.astype(jnp.float32)]
    dynamic_slice x0 -> x2, local copies, waits for them, and re-layouts: none -> 69.4 us  [exchange_in_pairs(): gathered = [blocks[position]]]
  transfers between devices with their start and end apart: 6 -> 10, of which waited for: 2 -> 4; matrix products, arithmetic and copies ran while one was open for 59% -> 33% of each run, Pallas kernels for 0% -> 0%
where the time goes in v1:
time: 2480 us; the launch traced here: 2460 us
  local copies, waits for them, and re-layouts  1120 us (45%)
  waiting for transfers between devices  387 us (16%)
  blocking collectives  381 us (15%)
  other arithmetic  375 us (15%)
  matrix products  150 us (6%)
  starting transfers between devices  35.7 us (1%)
    all_to_all x2, waiting for transfers between devices, body(): lax.all_to_all(flipped, 'dn', split_axis=1, concat_axis=0, tiled=True)  321 us
    convert_element_type x9, local copies, waits for them, and re-layouts, hop_lead(): return result.reshape(layout).astype(jnp.bfloat16)  266 us
    all_to_all x2, blocking collectives, body(): lax.all_to_all(cube, 'up', split_axis=1, concat_axis=0, tiled=True)  254 us
    convert_element_type x2, other arithmetic, hop_lead(): return result.reshape(layout).astype(jnp.bfloat16)  175 us
    unnamed x34, local copies, waits for them, and re-layouts  140 us
    another operation x8, local copies, waits for them, and re-layouts, hop_lead(): cube = matrix.reshape(layout[0] // tile_width, tile_width, -1)  123 us
    dot_general x4, matrix products, hop_lead(): jnp.einsum('ikab,ikbm->iam', signed, picked, preferred_element_type=jnp.f...  118 us
    gather x4, local copies, waits for them, and re-layouts, hop_lead(): picked = cube[tile_columns]  106 us
  transfers between devices with their start and end apart: 10, of which 4 were waited for; matrix products, arithmetic and copies ran while one was open for 33% of the time, Pallas kernels for 0%

profile of v1, /device:TPU:12, one launch (start us, length us, event | category | flops | bytes accessed | tf_op | source)
XLA Modules:
  0.0 2461.3 jit_solution(4745952599338156264)
XLA Ops:
  11.1 41.6 %psum.35 = f32[]{:T(128)} all-reduce(f32[]{:T(128)} %fusion), channel_id=1, replica_groups=mesh['up'=8,'dn'=4] {'up','dn'}, use_global_device_ids=true, to_apply=%region_1.0 | all-reduce | flops 1 | bytes 8 | tf_op jit(solution)/shard_map/psum | solution.py:55
  80.3 127.0 %all_to_all.78 = bf16[1664,8,416]{0,2,1:T(8,128)(2,1)} all-to-all(bf16[1664,8,416]{0,2,1:T(8,128)(2,1)} %bitcast.152), channel_id=1, replica_groups=mesh['up'=8,'dn'=4] {'up'}, dimensions={1} | all-to-all | bytes 22151168 | tf_op jit(solution)/shard_map/all_to_all | solution.py:65
  233.4 21.0 reshape_reshape.16
  265.3 26.4 %gather_fusion = bf16[520,128,416]{1,2,0:T(8,128)(2,1)} fusion(bf16[104,128,416]{1,2,0:T(8,128)(2,1)} %copy.77, s32[1024]{0:T(1024)S(1)} %pad_clamp_fusion.1), kind=kCustom, calls=%fused_computation | custom fusion | bytes 110757920 | tf_op jit(solution)/shard_map/gather | solution.py:36
  291.7 160.1 %all-to-all-done.2 = bf16[3328,4,416]{0,2,1:T(8,128)(2,1)} async-done(((bf16[3328,4,416]{0,2,1:T(8,128)(2,1)}), bf16[3328,4,416]{0,2,1:T(8,128)(2,1)}, u32[]{:S(2)}, u32[]{:S(2)}) %all-to-all-start.2) | async-done | bytes 11075616 | tf_op jit(solution)/shard_map/all_to_all | solution.py:71
  451.8 25.9 %copy.82 = bf16[4,3328,1,416]{1,0,3,2:T(4,128)(2,1)} copy(bf16[4,3328,1,416]{1,3,0,2:T(8,128)(2,1)} %bitcast.11) | data formatting | bytes 22151168 | tf_op jit(solution)/shard_map/all_to_all | solution.py:71
  477.7 18.8 reshape_reshape.17
  507.2 26.7 %gather_fusion.1 = bf16[520,128,416]{1,2,0:T(8,128)(2,1)} fusion(bf16[104,128,416]{1,2,0:T(8,128)(2,1)} %copy.83, s32[1024]{0:T(1024)S(1)} %pad_clamp_fusion.1), kind=kCustom, calls=%fused_computation.1 | custom fusion | bytes 110757920 | tf_op jit(solution)/shard_map/gather | solution.py:36
  533.8 29.4 %bitcast_convert_fusion.2 = bf16[104,128,416]{1,2,0:T(8,128)(2,1)} fusion(bf16[104,5,128,416]{2,3,1,0:T(8,128)(2,1)} %bitcast.149, bf16[104,5,128,128]{3,2,1,0:T(8,128)(2,1)} %param.6, bf16[104,5]{1,0:T(8,128)(2,1)S(1)} %copy.73), kind=kOutput, calls=%fused_computation.18 | convolution fusion | flops 7102431232 | bytes 83493904 | tf_op jit(solution)/shard_map/ikab,ikbm->iam/dot_general | solution.py:37
  563.3 19.5 copy.84
  582.8 19.4 convert_element_type.131
  602.2 34.7 %constant_dynamic-slice_fusion.7 = (bf16[1,3328,1,416]{1,0,3,2:T(2,128)(2,1)}, bf16[1,3328,1,416]{1,0,3,2:T(2,128)(2,1)}, bf16[1,3328,1,416]{1,0,3,2:T(2,128)(2,1)}, bf16[1,3328,1,416]{1,0,3,2:T(2,128)(2,1)}) fusion(bf16[4,3328,1,416]{1,0,3,2:T(4,128)(2,1)} %convert_element_type.131, s32[]{:T(128)S(6)} %select_n.40, s32[]{:T(128)S(6)} %select_n.43, ...), kind=kLoop, calls=%fused_computation.68 | loop fusion | bytes 22151184 | tf_op jit(solution)/shard_map/dynamic_slice | solution.py:24
  651.2 29.4 %bitcast_convert_fusion.3 = bf16[104,128,416]{1,2,0:T(8,128)(2,1)} fusion(bf16[104,5,128,416]{2,3,1,0:T(8,128)(2,1)} %bitcast.147, bf16[104,5,128,128]{3,2,1,0:T(8,128)(2,1)} %param.6, bf16[104,5]{1,0:T(8,128)(2,1)S(1)} %copy.73), kind=kOutput, calls=%fused_computation.19 | convolution fusion | flops 7102431232 | bytes 83493904 | tf_op jit(solution)/shard_map/ikab,ikbm->iam/dot_general | solution.py:37
  696.9 77.6 %reshape.199 = bf16[13312,1,416]{2,1,0:T(2,128)(2,1)} reshape(bf16[104,128,416]{2,1,0:T(8,128)(2,1)} %copy.111) | data formatting | bytes 22151168 | tf_op jit(solution)/shard_map/convert_element_type | solution.py:38
  775.0 87.5 %reduce = bf16[13312,416]{1,0:T(8,128)(2,1)} reduce(bf16[13312,1,416]{2,1,0:T(2,128)(2,1)} %reshape.199, bf16[]{:T(256)} %broadcast.62), dimensions={1}, to_apply=%reshape.199.reduce_sub_computation | reduce | bytes 22151170 | tf_op jit(solution)/shard_map/convert_element_type | solution.py:38
  862.5 21.7 reshape.201
  917.8 28.0 %pad_maximum_fusion = bf16[4,3328,1,416]{1,0,3,2:T(4,128)(2,1)S(1)} fusion(bf16[1,3328,1,416]{1,0,3,2:T(2,128)(2,1)} %copy.87, bf16[1,3328,1,416]{1,0,3,2:T(2,128)(2,1)} %copy.86, bf16[1,3328,1,416]{1,0,3,2:T(2,128)(2,1)} %copy.85, bf16[1,3328,1,416]{1,0,3,2:T(2,128)(2,1)} %get-tuple-element.23), kind=kLoop, calls=%fused_computation.26 | loop fusion | flops 44302336 | bytes 22151168 | tf_op jit(solution)/shard_map/stack | solution.py:28
  974.3 37.9 %all-to-all-done.1 = bf16[8,2,346112]{2,1,0:T(2,128)(2,1)} async-done(((bf16[8,2,346112]{2,1,0:T(2,128)(2,1)}), bf16[8,2,346112]{2,1,0:T(2,128)(2,1)}, u32[]{:S(2)}, u32[]{:S(2)}) %all-to-all-start.1) | async-done | bytes 11075616 | tf_op jit(solution)/shard_map/all_to_all | solution.py:68
  1012.1 30.4 %reshape.202 = bf16[13312,1,416]{2,1,0:T(2,128)(2,1)} reshape(bf16[8,2,346112]{2,1,0:T(2,128)(2,1)} %all-to-all-done.1) | data formatting | bytes 22151168
  1042.5 52.5 %copy.80 = bf16[13312,1,416]{0,2,1:T(8,128)(2,1)} copy(bf16[13312,1,416]{2,1,0:T(2,128)(2,1)} %reshape.202) | data formatting | bytes 22151168 | tf_op jit(solution)/shard_map/all_to_all | solution.py:68
  1110.3 19.8 copy.81
  1130.0 22.8 copy.90
  1165.4 32.2 %multiply_reduce_fusion.3 = (f32[]{:T(128)}, f32[]{:T(128)}, f32[1664,3328]{1,0:T(8,128)}, f32[1664,3328]{1,0:T(8,128)}) fusion(f32[]{:T(128)S(6)} %max.13, bf16[1664,3328]{1,0:T(8,128)(2,1)} %param.5, f32[1664,3328]{1,0:T(8,128)} %copy.90, f32[4,3328,1,416]{1,3,0,2:T(8,128)} %maximum_convert_fusion, s32[16,13312]{1,0:T(8,128)} %param.9, s32[]{:T(128)S(6)} %select_n.46, ...), kind=kOutput, calls=%fused_computation.25 | convolution fusion | flops 232667136 | bytes 99999760 | tf_op jit(solution)/shard_map/sa,sb->ab/dot_general | solution.py:51
  1197.6 42.7 %all-reduce.1 = (f32[]{:T(128)}, f32[]{:T(128)}) all-reduce(f32[]{:T(128)} %get-tuple-element.6, f32[]{:T(128)} %get-tuple-element.5), channel_id=1, replica_groups=mesh['up'=8,'dn'=4] {'up','dn'}, use_global_device_ids=true, to_apply=%region_5.0 | all-reduce | flops 2 | bytes 16 | tf_op jit(solution)/shard_map/psum | solution.py:82
  1243.5 22.7 fusion.29
  1282.5 127.0 %all_to_all.79 = bf16[1664,8,416]{0,2,1:T(8,128)(2,1)} all-to-all(bf16[1664,8,416]{0,2,1:T(8,128)(2,1)} %bitcast.153), channel_id=1, replica_groups=mesh['up'=8,'dn'=4] {'up'}, dimensions={1} | all-to-all | bytes 22151168 | tf_op jit(solution)/shard_map/all_to_all | solution.py:65
  1434.6 21.0 reshape_reshape.18
  1466.4 26.4 %gather_fusion.2 = bf16[520,128,416]{1,2,0:T(8,128)(2,1)} fusion(bf16[104,128,416]{1,2,0:T(8,128)(2,1)} %copy.93, s32[1024]{0:T(1024)S(1)} %copy-done.1), kind=kCustom, calls=%fused_computation.2 | custom fusion | bytes 110757920 | tf_op jit(solution)/shard_map/gather | solution.py:36
  1492.9 160.9 %all-to-all-done.5 = bf16[3328,4,416]{0,2,1:T(8,128)(2,1)} async-done(((bf16[3328,4,416]{0,2,1:T(8,128)(2,1)}), bf16[3328,4,416]{0,2,1:T(8,128)(2,1)}, u32[]{:S(2)}, u32[]{:S(2)}) %all-to-all-start.5) | async-done | bytes 11075616 | tf_op jit(solution)/shard_map/all_to_all | solution.py:71
  1653.7 25.9 %copy.98 = bf16[4,3328,1,416]{1,0,3,2:T(4,128)(2,1)} copy(bf16[4,3328,1,416]{1,3,0,2:T(8,128)(2,1)} %bitcast.37) | data formatting | bytes 22151168 | tf_op jit(solution)/shard_map/all_to_all | solution.py:71
  1709.1 26.7 %gather_fusion.3 = bf16[520,128,416]{1,2,0:T(8,128)(2,1)} fusion(bf16[104,128,416]{1,2,0:T(8,128)(2,1)} %copy.99, s32[1024]{0:T(1024)S(1)} %copy-done.1), kind=kCustom, calls=%fused_computation.3 | custom fusion | bytes 110757920 | tf_op jit(solution)/shard_map/gather | solution.py:36
  1735.8 29.4 %bitcast_convert_fusion = bf16[104,128,416]{1,2,0:T(8,128)(2,1)} fusion(bf16[104,5,128,416]{2,3,1,0:T(8,128)(2,1)} %bitcast.148, bf16[104,5,128,128]{3,2,1,0:T(8,128)(2,1)} %param.6, bf16[104,5]{1,0:T(8,128)(2,1)S(1)} %copy-done.3), kind=kOutput, calls=%fused_computation.16 | convolution fusion | flops 7102431232 | bytes 83493904 | tf_op jit(solution)/shard_map/ikab,ikbm->iam/dot_general | solution.py:37
  1765.2 19.5 copy.100
  1784.8 19.4 convert_element_type.146
  1804.2 34.7 %constant_dynamic-slice_fusion.2 = (bf16[1,3328,1,416]{1,0,3,2:T(2,128)(2,1)}, bf16[1,3328,1,416]{1,0,3,2:T(2,128)(2,1)}, bf16[1,3328,1,416]{1,0,3,2:T(2,128)(2,1)}, bf16[1,3328,1,416]{1,0,3,2:T(2,128)(2,1)}) fusion(bf16[4,3328,1,416]{1,0,3,2:T(4,128)(2,1)} %convert_element_type.146, s32[]{:T(128)S(6)} %select_n.40, s32[]{:T(128)S(6)} %select_n.43, ...), kind=kLoop, calls=%fused_computation.62 | loop fusion | bytes 22151184 | tf_op jit(solution)/shard_map/dynamic_slice | solution.py:24
  1852.5 29.4 %bitcast_convert_fusion.1 = bf16[104,128,416]{1,2,0:T(8,128)(2,1)} fusion(bf16[104,5,128,416]{2,3,1,0:T(8,128)(2,1)} %bitcast.146, bf16[104,5,128,128]{3,2,1,0:T(8,128)(2,1)} %param.6, bf16[104,5]{1,0:T(8,128)(2,1)S(1)} %copy-done.3), kind=kOutput, calls=%fused_computation.17 | convolution fusion | flops 7102431232 | bytes 83493904 | tf_op jit(solution)/shard_map/ikab,ikbm->iam/dot_general | solution.py:37
  1898.2 77.6 %reshape.200 = bf16[13312,1,416]{2,1,0:T(2,128)(2,1)} reshape(bf16[104,128,416]{2,1,0:T(8,128)(2,1)} %copy.112) | data formatting | bytes 22151168 | tf_op jit(solution)/shard_map/convert_element_type | solution.py:38
  1975.8 87.5 %reduce.1 = bf16[13312,416]{1,0:T(8,128)(2,1)} reduce(bf16[13312,1,416]{2,1,0:T(2,128)(2,1)} %reshape.200, bf16[]{:T(256)} %broadcast.62), dimensions={1}, to_apply=%reshape.200.reduce_sub_computation | reduce | bytes 22151170 | tf_op jit(solution)/shard_map/convert_element_type | solution.py:38
  2063.3 21.7 reshape.203
  2117.4 28.0 %pad_maximum_fusion.1 = bf16[4,3328,1,416]{1,0,3,2:T(4,128)(2,1)S(1)} fusion(bf16[1,3328,1,416]{1,0,3,2:T(2,128)(2,1)} %copy.103, bf16[1,3328,1,416]{1,0,3,2:T(2,128)(2,1)} %copy.102, bf16[1,3328,1,416]{1,0,3,2:T(2,128)(2,1)} %copy.101, bf16[1,3328,1,416]{1,0,3,2:T(2,128)(2,1)} %get-tuple-element.17), kind=kLoop, calls=%fused_computation.28 | loop fusion | flops 44302336 | bytes 22151168 | tf_op jit(solution)/shard_map/stack | solution.py:28
  2184.4 28.5 %all-to-all-done.4 = bf16[8,2,346112]{2,1,0:T(2,128)(2,1)} async-done(((bf16[8,2,346112]{2,1,0:T(2,128)(2,1)}), bf16[8,2,346112]{2,1,0:T(2,128)(2,1)}, u32[]{:S(2)}, u32[]{:S(2)}) %all-to-all-start.4) | async-done | bytes 11075616 | tf_op jit(solution)/shard_map/all_to_all | solution.py:68
  2213.0 30.4 %reshape.204 = bf16[13312,1,416]{2,1,0:T(2,128)(2,1)} reshape(bf16[8,2,346112]{2,1,0:T(2,128)(2,1)} %all-to-all-done.4) | data formatting | bytes 22151168
  2243.4 52.5 %copy.96 = bf16[13312,1,416]{0,2,1:T(8,128)(2,1)} copy(bf16[13312,1,416]{2,1,0:T(2,128)(2,1)} %reshape.204) | data formatting | bytes 22151168 | tf_op jit(solution)/shard_map/all_to_all | solution.py:68
  2311.3 19.4 copy.97
  2330.7 22.8 copy.106
  2353.5 40.2 %multiply_reduce_fusion.1 = (f32[]{:T(128)}, f32[]{:T(128)}, f32[1664,3328]{1,0:T(8,128)}) fusion(f32[1664,3328]{1,0:T(8,128)} %get-tuple-element.13, f32[]{:T(128)S(6)} %max.13, bf16[1664,3328]{1,0:T(8,128)(2,1)} %param.5, f32[]{:T(128)} %sqrt.10, f32[1664,3328]{1,0:T(8,128)} %get-tuple-element.27, f32[1664,3328]{1,0:T(8,128)} %copy.106, ...), kind=kLoop, calls=%fused_computation.22 | loop fusion | flops 66453504 | bytes 121831440 | tf_op jit(solution)/shard_map/reduce_sum | solution.py:82
  2393.8 42.6 %all-reduce = (f32[]{:T(128)}, f32[]{:T(128)}) all-reduce(f32[]{:T(128)} %get-tuple-element.4, f32[]{:T(128)} %get-tuple-element.3), channel_id=1, replica_groups=mesh['up'=8,'dn'=4] {'up','dn'}, use_global_device_ids=true, to_apply=%region_9.0 | all-reduce | flops 2 | bytes 16 | tf_op jit(solution)/shard_map/psum | solution.py:82
  2439.3 19.4 divide_convert_fusion
  (91 shorter events, 405.2 us)
Async XLA Ops:
  207.3 6.9 copy-start.6
  207.3 7.2 copy-start.5
  207.3 244.4 %all-to-all-start.2 = ((bf16[3328,4,416]{0,2,1:T(8,128)(2,1)}), bf16[3328,4,416]{0,2,1:T(8,128)(2,1)}, u32[]{:S(2)}, u32[]{:S(2)}) async-start(bf16[3328,4,416]{0,2,1:T(8,128)(2,1)} %bitcast.138), calls=%async_computation.2 | async-start | bytes 22151168 | tf_op jit(solution)/shard_map/all_to_all | solution.py:71
  214.6 436.5 %copy-start.2 = (bf16[104,5]{1,0:T(8,128)(2,1)}, bf16[104,5]{1,0:T(8,128)(2,1)S(1)}, u32[]{:S(2)}) copy-start(bf16[104,5]{1,0:T(8,128)(2,1)S(1)} %copy.73) | copy-start | bytes 3124
  214.7 292.5 %copy-start = (s32[1024]{0:T(1024)}, s32[1024]{0:T(1024)S(1)}, u32[]{:S(2)}) copy-start(s32[1024]{0:T(1024)S(1)} %pad_clamp_fusion.1) | copy-start | bytes 12292
  636.9 11.0 slice-start.2
  639.9 7.9 slice-start.3
  639.9 252.2 %collective-permute-start = (bf16[3328,1,416]{0,2,1:T(8,128)(2,1)S(1)}, bf16[3328,1,416]{0,2,1:T(8,128)(2,1)}, u32[]{:S(2)}, u32[]{:S(2)}) collective-permute-start(bf16[3328,1,416]{0,2,1:T(8,128)(2,1)S(1)} %bitcast.164), channel_id=1, source_target_pairs={{0,1},{1,0},{2,3},{3,2},{4,5},{5,4},{6,7},{7,6},{8,9},{9,8},{10,11... | collective-permute-start | bytes 8306696 | tf_op jit(solution)/shard_map/ppermute | solution.py:27
  647.8 252.9 %collective-permute-start.1 = (bf16[3328,1,416]{0,2,1:T(8,128)(2,1)}, bf16[3328,1,416]{0,2,1:T(8,128)(2,1)}, u32[]{:S(2)}, u32[]{:S(2)}) collective-permute-start(bf16[3328,1,416]{0,2,1:T(8,128)(2,1)} %bitcast.136), channel_id=1, source_target_pairs={{0,2},{1,3},{2,0},{3,1},{4,6},{5,7},{6,4},{7,5},{8,10},{9,11},{10,... | collective-permute-start | bytes 8306696 | tf_op jit(solution)/shard_map/ppermute | solution.py:27
  649.7 259.4 %collective-permute-start.2 = (bf16[3328,1,416]{0,2,1:T(8,128)(2,1)}, bf16[3328,1,416]{0,2,1:T(8,128)(2,1)}, u32[]{:S(2)}, u32[]{:S(2)}) collective-permute-start(bf16[3328,1,416]{0,2,1:T(8,128)(2,1)} %bitcast.135), channel_id=1, source_target_pairs={{0,3},{1,2},{2,1},{3,0},{4,7},{5,6},{6,5},{7,4},{8,11},{9,10},{10,... | collective-permute-start | bytes 8306696 | tf_op jit(solution)/shard_map/ppermute | solution.py:27
  884.2 127.9 %all-to-all-start.1 = ((bf16[8,2,346112]{2,1,0:T(2,128)(2,1)}), bf16[8,2,346112]{2,1,0:T(2,128)(2,1)}, u32[]{:S(2)}, u32[]{:S(2)}) async-start(bf16[8,2,346112]{2,1,0:T(2,128)(2,1)} %reshape.201), calls=%async_computation.1 | async-start | bytes 22151168 | tf_op jit(solution)/shard_map/all_to_all | solution.py:68
  892.2 75.9 %copy-start.4 = (s32[1024]{0:T(1024)}, s32[1024]{0:T(1024)S(1)}, u32[]{:S(2)}) copy-start(s32[1024]{0:T(1024)S(1)} %pad_clamp_fusion) | copy-start | bytes 12292
  1409.6 244.2 %all-to-all-start.5 = ((bf16[3328,4,416]{0,2,1:T(8,128)(2,1)}), bf16[3328,4,416]{0,2,1:T(8,128)(2,1)}, u32[]{:S(2)}, u32[]{:S(2)}) async-start(bf16[3328,4,416]{0,2,1:T(8,128)(2,1)} %bitcast.139), calls=%async_computation.5 | async-start | bytes 22151168 | tf_op jit(solution)/shard_map/all_to_all | solution.py:71
  1455.6 10.8 copy-start.1
  1709.1 26.7 %copy-start.3 = (bf16[104,5]{1,0:T(8,128)(2,1)S(1)}, bf16[104,5]{1,0:T(8,128)(2,1)}, u32[]{:S(2)}) copy-start(bf16[104,5]{1,0:T(8,128)(2,1)} %copy-done.2) | copy-start | bytes 3124
  1838.9 11.0 slice-start
  1842.0 8.0 slice-start.1
  1842.0 249.7 %collective-permute-start.3 = (bf16[3328,1,416]{0,2,1:T(8,128)(2,1)S(1)}, bf16[3328,1,416]{0,2,1:T(8,128)(2,1)}, u32[]{:S(2)}, u32[]{:S(2)}) collective-permute-start(bf16[3328,1,416]{0,2,1:T(8,128)(2,1)S(1)} %bitcast.165), channel_id=1, source_target_pairs={{0,1},{1,0},{2,3},{3,2},{4,5},{5,4},{6,7},{7,6},{8,9},{9,8},{10,11... | collective-permute-start | bytes 8306696 | tf_op jit(solution)/shard_map/ppermute | solution.py:27
  1849.1 251.1 %collective-permute-start.4 = (bf16[3328,1,416]{0,2,1:T(8,128)(2,1)}, bf16[3328,1,416]{0,2,1:T(8,128)(2,1)}, u32[]{:S(2)}, u32[]{:S(2)}) collective-permute-start(bf16[3328,1,416]{0,2,1:T(8,128)(2,1)} %bitcast.133), channel_id=1, source_target_pairs={{0,2},{1,3},{2,0},{3,1},{4,6},{5,7},{6,4},{7,5},{8,10},{9,11},{10,... | collective-permute-start | bytes 8306696 | tf_op jit(solution)/shard_map/ppermute | solution.py:27
  1851.8 256.8 %collective-permute-start.5 = (bf16[3328,1,416]{0,2,1:T(8,128)(2,1)}, bf16[3328,1,416]{0,2,1:T(8,128)(2,1)}, u32[]{:S(2)}, u32[]{:S(2)}) collective-permute-start(bf16[3328,1,416]{0,2,1:T(8,128)(2,1)} %bitcast.132), channel_id=1, source_target_pairs={{0,3},{1,2},{2,1},{3,0},{4,7},{5,6},{6,5},{7,4},{8,11},{9,10},{10,... | collective-permute-start | bytes 8306696 | tf_op jit(solution)/shard_map/ppermute | solution.py:27
  2085.0 128.0 %all-to-all-start.4 = ((bf16[8,2,346112]{2,1,0:T(2,128)(2,1)}), bf16[8,2,346112]{2,1,0:T(2,128)(2,1)}, u32[]{:S(2)}, u32[]{:S(2)}) async-start(bf16[8,2,346112]{2,1,0:T(2,128)(2,1)} %reshape.203), calls=%async_computation.4 | async-start | bytes 22151168 | tf_op jit(solution)/shard_map/all_to_all | solution.py:68
